TPU v7x, 32 devices: a whole 2x2x4 slice. The times are simulated.
32 devices in a mesh: sample: 8 (over y, x, core), line: 4 (over z).
Axes of the slice: x: 2, y: 2, z: 4, core: 2. Of those that a mesh axis runs over, the one named last changes fastest.
Arguments:
- wind_dev: bfloat16 [4096, 10000], P('sample', 'line'), may hold values from -6 to 6
- ptdf: bfloat16 [4096, 10000], P('line'), may hold values from -0.0625 to 0.0625
- region_weights: bfloat16 [31, 10000], replicated, may hold values from -0.0625 to 0.0625
- incidence: int32 [12706, 2], replicated, may hold values from 0 to 9999
- monitored: int32 [4096], P('line'), may hold values from 0 to 12705
- ratings: float32 [12706], replicated, may hold values from 1 to 3
- base_flow: float32 [4096], P('line'), may hold values from -6 to 6
- line_cost: float32 [4096], P('line'), may hold values from 0.2 to 20
- policy: float32 [32, 4096], P(None, 'line'), may hold values from -0.6 to 0.6
Outputs:
- new_policy: float32 [32, 4096], P(None, 'line')
- new_flows: float32 [4096, 4096], P('sample', 'line')
- decrement: float32 [], replicated
- grad_norm: float32 [], replicated
All inputs are finite; a program needn't handle non-finite values.
Results may differ from a plain program's by a relative error of at most 0.0003.
Values may be sent and summed in bfloat16 or wider, within the bound.
A program may use at most 128 MiB of HBM per device.

v0:
```python
import jax
import jax.numpy as jnp
from jax import lax
from jax.sharding import PartitionSpec as P

ridge_weight = 1.0
barrier_weight = 0.1
smoothing = 0.5


def penalty_terms(factors, ends_diff, slope_term, curve_term, weight):
    highest = lax.Precision.HIGHEST
    regions = factors.shape[1]
    lines_here = slope_term.shape[1]
    outer_prod = (factors[:, :, None] * factors[:, None, :]).reshape(
        factors.shape[0], regions * regions
    )
    block_rr = lax.dot_general(outer_prod, curve_term, (((0,), (0,)), ((), ())), precision=highest)
    weighted = curve_term * ends_diff
    cross_re = lax.dot_general(factors, weighted, (((0,), (0,)), ((), ())), precision=highest)
    corner = jnp.sum(weighted * ends_diff, axis=0)
    upper_rows = jnp.concatenate(
        [block_rr.reshape(regions, regions, lines_here), cross_re[:, None, :]], axis=1
    )
    bottom = jnp.concatenate([cross_re[None, :, :], corner[None, None, :]], axis=1)
    hessian = jnp.concatenate([upper_rows, bottom], axis=0) * weight
    grad_rr = lax.dot_general(factors, slope_term, (((0,), (0,)), ((), ())), precision=highest)
    gradient = (
        jnp.concatenate([grad_rr, jnp.sum(slope_term * ends_diff, axis=0)[None, :]], axis=0)
        * weight
    )
    return (hessian.reshape((regions + 1) * (regions + 1), lines_here), gradient)


def factor_solve(hessian, gradient):
    features = gradient.shape[0]
    positions = jnp.arange(features, dtype=jnp.int32)

    def chol_column(column, lower_tri):
        target = lax.dynamic_index_in_dim(hessian, column, 1, keepdims=False)
        row_here = lax.dynamic_index_in_dim(lower_tri, column, 0, keepdims=False)
        running = target - jnp.sum(lower_tri * row_here[None, :, :], axis=1)
        pivot_val = jnp.sqrt(lax.dynamic_index_in_dim(running, column, 0, keepdims=False))
        new_col = jnp.where(
            (positions >= column)[:, None], running / pivot_val[None, :], jnp.zeros_like(running)
        )
        select = (positions == column).astype(hessian.dtype)
        return lower_tri + new_col[:, None, :] * select[None, :, None]

    lower_tri = lax.fori_loop(0, features, chol_column, jnp.zeros_like(hessian))

    def forward_row(row_index, forward):
        row_here = lax.dynamic_index_in_dim(lower_tri, row_index, 0, keepdims=False)
        running = lax.dynamic_index_in_dim(gradient, row_index, 0, keepdims=False) - jnp.sum(
            row_here * forward, axis=0
        )
        value = running / lax.dynamic_index_in_dim(row_here, row_index, 0, keepdims=False)
        select = (positions == row_index).astype(gradient.dtype)
        return forward + select[:, None] * value[None, :]

    forward = lax.fori_loop(0, features, forward_row, jnp.zeros_like(gradient))

    def backward_row(turn, backward):
        row_index = features - 1 - turn
        col_here = lax.dynamic_index_in_dim(lower_tri, row_index, 1, keepdims=False)
        running = lax.dynamic_index_in_dim(forward, row_index, 0, keepdims=False) - jnp.sum(
            col_here * backward, axis=0
        )
        value = running / lax.dynamic_index_in_dim(col_here, row_index, 0, keepdims=False)
        select = (positions == row_index).astype(gradient.dtype)
        return backward + select[:, None] * value[None, :]

    backward = lax.fori_loop(0, features, backward_row, jnp.zeros_like(gradient))
    return (forward, -backward)


def owner_step(hessian_flat, gradient, policy_part):
    features = gradient.shape[0]
    lines_here = gradient.shape[1]
    hessian = hessian_flat.reshape(features, features, lines_here)
    margin_sq = 1.0 - policy_part * policy_part
    diag_terms = ridge_weight + barrier_weight * 2.0 * (1.0 + policy_part * policy_part) / (
        margin_sq * margin_sq
    )
    hessian = hessian + jnp.eye(features, dtype=hessian.dtype)[:, :, None] * diag_terms[:, None, :]
    gradient = (
        gradient + ridge_weight * policy_part + barrier_weight * 2.0 * policy_part / margin_sq
    )
    forward, newton_step = factor_solve(hessian, gradient)
    return (gradient, forward, newton_step)


def shards(
    wind_dev, ptdf, region_weights, incidence, monitored, ratings, base_flow, line_cost, policy
):
    highest = lax.Precision.HIGHEST
    regions = region_weights.shape[0]
    endpoints = jnp.take(incidence, monitored, axis=0)
    from_bus = endpoints[:, 0]
    to_bus = endpoints[:, 1]
    rating = jnp.take(ratings, monitored)
    scen_here = wind_dev.shape[0]
    lines_here = ptdf.shape[0]

    def pick_buses(wind_piece, bus_ids):
        piece_width = wind_piece.shape[1]
        inside = (bus_ids >= 0) & (bus_ids < piece_width)
        picked = jnp.take(wind_piece, jnp.clip(bus_ids, 0, piece_width - 1), axis=1).astype(
            jnp.float32
        )
        return jnp.where(inside[None, :], picked, 0.0)

    wind_piece = lax.all_gather(wind_dev, "line", axis=1, tiled=True)
    grid_flow = lax.dot_general(
        wind_piece, ptdf, (((1,), (1,)), ((), ())), preferred_element_type=jnp.float32
    )
    ends_diff = pick_buses(wind_piece, to_bus) - pick_buses(wind_piece, from_bus)
    grid_flow, ends_diff = (grid_flow, ends_diff)
    factors = lax.dot_general(
        wind_piece, region_weights, (((1,), (1,)), ((), ())), preferred_element_type=jnp.float32
    )
    grid_flow, ends_diff, folded_factors = (grid_flow, ends_diff, factors)
    factors = folded_factors
    line_flow = (
        grid_flow
        + base_flow[None, :]
        + jnp.dot(factors, policy[:regions], precision=highest)
        + policy[regions][None, :] * ends_diff
    )
    prob_up = jax.nn.sigmoid((line_flow - rating[None, :]) / smoothing)
    prob_down = jax.nn.sigmoid((-line_flow - rating[None, :]) / smoothing)
    slope_term = prob_up - prob_down
    curve_term = (prob_up * (1.0 - prob_up) + prob_down * (1.0 - prob_down)) / smoothing
    weight = line_cost / (scen_here * lax.axis_size("sample"))
    hessian_part, gradient_part = penalty_terms(factors, ends_diff, slope_term, curve_term, weight)
    hessian_sum, gradient_sum = (
        lax.psum_scatter(hessian_part, "sample", scatter_dimension=1, tiled=True),
        lax.psum_scatter(gradient_part, "sample", scatter_dimension=1, tiled=True),
    )
    share_width = gradient_sum.shape[1]
    policy_share = lax.dynamic_slice_in_dim(
        policy, lax.axis_index("sample") * share_width, share_width, 1
    )
    gradient, forward, newton_step = owner_step(hessian_sum, gradient_sum, policy_share)
    decrement_sq, norm_sq = lax.psum(
        (jnp.sum(forward * forward), jnp.sum(gradient * gradient)), ("sample", "line")
    )
    full_step = lax.all_gather(newton_step, "sample", axis=1, tiled=True)
    total_lines = lines_here * lax.axis_size("line")
    features = policy.shape[0]
    step_length = 1.0 / (1.0 + jnp.sqrt(decrement_sq / (barrier_weight * features * total_lines)))
    new_policy = policy + step_length * full_step
    shift_flow = (
        jnp.dot(factors, full_step[:regions], precision=highest)
        + full_step[regions][None, :] * ends_diff
    )
    new_flows = line_flow + step_length * shift_flow
    return (new_policy, new_flows, jnp.sqrt(decrement_sq), jnp.sqrt(norm_sq))


def solution(mesh):
    placed = (
        P("sample", "line"),
        P("line", None),
        P(),
        P(),
        P("line"),
        P(),
        P("line"),
        P("line"),
        P(None, "line"),
    )
    return jax.shard_map(
        shards,
        mesh=mesh,
        in_specs=placed,
        out_specs=(P(None, "line"), P("sample", "line"), P(), P()),
        check_vma=False,
    )
```

profile of v0, /device:TPU:0, one launch (start us, length us, event | category | flops | bytes accessed | tf_op | source)
XLA Modules:
  0.0 437.1 jit_solution(4000536996957943662)
XLA Ops:
  8.1 4.1 copy.20
  12.3 5.7 %gather_fusion = s32[1024,2]{1,0:T(8,128)S(1)} fusion(s32[12706,2]{1,0:T(8,128)} %copy.20, s32[1024]{0:T(1024)S(1)} %fusion.32), kind=kCustom, calls=%fused_computation.2 | custom fusion | bytes 20480 | tf_op jit(solution)/shard_map/jit(_take)/gather | solution.py:98
  18.0 6.2 %gather_fusion.1 = f32[1024]{0:T(1024)S(1)} fusion(f32[12706]{0:T(1024)S(1)} %copy-done.2, s32[1024]{0:T(1024)S(1)} %fusion.32), kind=kCustom, calls=%fused_computation.3 | custom fusion | bytes 12288 | tf_op jit(solution)/shard_map/jit(_take)/gather | solution.py:101
  25.5 167.0 %all-gather.3.cloned.1.call-done = bf16[4,2500,512]{2,1,0:T(8,128)(2,1)} async-done(((bf16[1,2500,512]{2,1,0:T(8,128)(2,1)}), bf16[4,2500,512]{2,1,0:T(8,128)(2,1)}) %all-gather.3.cloned.1.call-update) | async-done | bytes 10240016 | tf_op jit(solution)/shard_map/all_gather | solution.py:113
  192.5 11.5 %reshape.198 = bf16[10000,512]{1,0:T(8,128)(2,1)} reshape(bf16[4,2500,512]{2,1,0:T(8,128)(2,1)} %all-gather.3.cloned.1.call-done) | data formatting | bytes 20480000
  203.9 9.2 %gather_fusion.3 = bf16[1024,512]{1,0:T(8,128)(2,1)S(1)} fusion(bf16[512,10000]{0,1:T(8,128)(2,1)} %bitcast.127, s32[1024]{0:T(1024)S(1)} %get-tuple-element.496), kind=kCustom, calls=%fused_computation.1.clone | custom fusion | bytes 2101248 | tf_op jit(solution)/shard_map/jit(_take)/gather | solution.py:108
  213.7 9.6 %gather_fusion.2 = bf16[1024,512]{1,0:T(8,128)(2,1)S(1)} fusion(bf16[512,10000]{0,1:T(8,128)(2,1)} %bitcast.128, s32[1024]{0:T(1024)S(1)} %get-tuple-element.495), kind=kCustom, calls=%fused_computation.clone | custom fusion | bytes 2101248 | tf_op jit(solution)/shard_map/jit(_take)/gather | solution.py:108
  224.7 5.7 %fusion.37 = f32[512,31]{0,1:T(8,128)S(1)} fusion(bf16[10000,512]{1,0:T(8,128)(2,1)} %reshape.198, bf16[31,10000]{1,0:T(8,128)(2,1)S(1)} %copy-done), kind=kOutput, calls=%fused_computation.90 | convolution fusion | flops 317440000 | bytes 10923488 | tf_op jit(solution)/shard_map/dot_general | solution.py:119
  230.3 17.1 %fusion.38 = f32[512,1024]{1,0:T(8,128)S(1)} fusion(bf16[10000,512]{1,0:T(8,128)(2,1)} %reshape.198, bf16[1024,10000]{0,1:T(8,128)(2,1)} %param.18), kind=kOutput, calls=%fused_computation.91 | convolution fusion | flops 10485760000 | bytes 32817152 | tf_op jit(solution)/shard_map/dot_general | solution.py:114
  247.5 4.3 multiply_reduce_fusion.2
  251.8 2.2 fusion.27
  254.0 3.3 fusion.25
  258.4 1.5 mul.325
  259.9 1.7 dot_general.30
  261.6 9.4 %fusion.23 = f32[31,31,1024]{2,1,0:T(8,128)S(1)} fusion(f32[31,31,512]{2,1,0:T(8,128)S(1)} %dot_general.30, f32[512,1024]{1,0:T(8,128)} %copy-done.12, f32[1024]{0:T(1024)S(1)} %get-tuple-element.487), kind=kOutput, calls=%fused_computation.49 | convolution fusion | flops 6055002112 | bytes 8005632 | tf_op jit(solution)/shard_map/dot_general | solution.py:18
  271.9 2.4 bitcast_multiply_fusion.1
  274.4 15.7 %reduce-scatter.3.cloned.1.call-done = f32[32,128]{1,0:T(8,128)} async-done(((f32[32,1024]{1,0:T(8,128)}), f32[32,128]{1,0:T(8,128)}) %reduce-scatter.3.cloned.1.call-update) | async-done | bytes 16400 | tf_op jit(solution)/shard_map/reduce_scatter | solution.py:138
  291.5 53.1 %reduce-scatter.5.cloned.1.call-done = f32[1024,128]{1,0:T(8,128)} async-done(((f32[1024,1024]{1,0:T(8,128)}), f32[1024,128]{1,0:T(8,128)}) %reduce-scatter.5.cloned.1.call-update) | async-done | bytes 524304 | tf_op jit(solution)/shard_map/reduce_scatter | solution.py:137
  345.8 15.0 %while.51 = (s32[]{:T(128)}, f32[32,32,128]{2,1,0:T(8,128)S(1)}, f32[32,32,128]{2,1,0:T(8,128)S(1)}, s32[]{:T(128)}, s32[]{:T(128)}) while((s32[]{:T(128)}, f32[32,32,128]{2,1,0:T(8,128)S(1)}, f32[32,32,128]{2,1,0:T(8,128)S(1)}, s32[]{:T(128)}, s32[]{:T(128)}) %tuple.130), condition=%wide.region_4.6_spmd.clone.clone, body=%wide.region_2.5_spmd.clone.clone.sunk | while | flops 925923 | bytes 2787745 | solution.py:50
  360.9 4.2 while.49
  365.7 5.2 %while.50 = (s32[]{:T(128)}, f32[32,128]{1,0:T(8,128)S(1)}, f32[32,128]{1,0:T(8,128)S(1)}, f32[32,32,128]{2,1,0:T(8,128)S(1)}, s32[]{:T(128)}, /*index=5*/s32[]{:T(128)}, s32[]{:T(128)}, s32[]{:T(128)}) while((s32[]{:T(128)}, f32[32,128]{1,0:T(8,128)S(1)}, f32[32,128]{1,0:T(8,128)S(1)}, f32[32,32,128]{2,1,0:T(8,128)S(1)}, ...), condition=%wide.region_14.16_spmd.clone, body=%wide.region_12.15_spmd.clone.sunk | while | flops 24776 | bytes 101814 | solution.py:73
  370.9 9.3 %all_gather.7 = f32[32,1024]{1,0:T(8,128)S(1)} all-gather(f32[32,128]{1,0:T(8,128)S(1)} %neg.15), channel_id=1, replica_groups=mesh['sample'=8,'line'=4] {'sample'}, dimensions={1}, use_global_device_ids=true | all-gather | bytes 147456 | tf_op jit(solution)/shard_map/all_gather | solution.py:148
  380.1 39.8 %all-reduce = (f32[]{:T(128)}, f32[]{:T(128)}) all-reduce(f32[]{:T(128)} %multiply_reduce_fusion.5, f32[]{:T(128)} %get-tuple-element.485), channel_id=1, replica_groups=mesh['sample'=8,'line'=4] {'sample','line'}, use_global_device_ids=true, to_apply=%region_11.13 | all-reduce | flops 2 | bytes 16 | tf_op jit(solution)/shard_map/psum | solution.py:145
  422.0 5.5 %multiply_add_fusion.3 = f32[512,1024]{1,0:T(8,128)} fusion(f32[512,1024]{1,0:T(8,128)} %copy-done.12, f32[512,31]{0,1:T(8,128)S(1)} %fusion.37, f32[1024]{0:T(1024)S(1)} %bitcast.139, f32[]{:T(128)S(6)} %div.86, f32[32,1024]{1,0:T(8,128)S(1)} %all_gather.7, bf16[1024,512]{0,1:T(8,128)(2,1)S(1)} %copy-done.4, pred[1024]{0:T(1024)(128)(4,1)S(1)} %get-tuple-element.493, ...), kind=kOutput, calls=%fused_computation.51 | convolution fusion | flops 200802304 | bytes 6494212 | tf_op jit(solution)/shard_map/dot_general | solution.py:154
  (601 shorter events, 31.0 us)
Async XLA Ops:
  7.2 217.5 %copy-start = (bf16[31,10000]{1,0:T(8,128)(2,1)S(1)}, bf16[31,10000]{1,0:T(8,128)(2,1)}, u32[]{:S(2)}) copy-start(bf16[31,10000]{1,0:T(8,128)(2,1)} %param.19) | copy-start | bytes 1860004
  7.2 1.0 copy-start.8
  7.2 185.3 %all-gather.3.cloned.1.call-start = ((), (), s32[]{:S(2)}) async-start(), calls=%async_computation.4 | async-start | bytes 12820480 | tf_op jit(solution)/shard_map/all_gather | solution.py:113
  7.9 4.3 copy-start.9
  7.9 282.2 %reduce-scatter.3.cloned.1.call-start = ((), (), s32[]{:S(2)}) async-start(), calls=%async_computation.2 | async-start | bytes 147456 | tf_op jit(solution)/shard_map/reduce_scatter | solution.py:138
  12.3 5.7 %copy-start.2 = (f32[12706]{0:T(1024)S(1)}, f32[12706]{0:T(1024)}, u32[]{:S(2)}) copy-start(f32[12706]{0:T(1024)} %param.22) | copy-start | bytes 152476
  18.0 6.2 %copy-start.7 = (f32[32,1024]{1,0:T(8,128)S(1)}, f32[32,1024]{1,0:T(8,128)}, u32[]{:S(2)}) copy-start(f32[32,1024]{1,0:T(8,128)} %param.25) | copy-start | bytes 393220
  24.1 1.3 copy-start.10
  213.7 40.3 %copy-start.3 = (bf16[1024,512]{0,1:T(8,128)(2,1)}, bf16[1024,512]{0,1:T(8,128)(2,1)S(1)}, u32[]{:S(2)}) copy-start(bf16[1024,512]{0,1:T(8,128)(2,1)S(1)} %copy.22) | copy-start | bytes 3145732
  230.3 17.1 %copy-start.5 = (bf16[1024,512]{0,1:T(8,128)(2,1)S(1)}, bf16[1024,512]{0,1:T(8,128)(2,1)}, u32[]{:S(2)}) copy-start(bf16[1024,512]{0,1:T(8,128)(2,1)} %copy.21) | copy-start | bytes 3145732
  230.3 17.1 %copy-start.11 = (f32[1024]{0:T(1024)S(1)}, f32[1024]{0:T(1024)}, u32[]{:S(2)}) copy-start(f32[1024]{0:T(1024)} %param.23) | copy-start | bytes 12292
  251.8 2.2 copy-start.12
  258.2 86.3 %reduce-scatter.5.cloned.1.call-start = ((), (), s32[]{:S(2)}) async-start(), calls=%async_computation.3 | async-start | bytes 4718592 | tf_op jit(solution)/shard_map/reduce_scatter | solution.py:137
  345.8 76.2 %copy-start.4 = (bf16[1024,512]{0,1:T(8,128)(2,1)S(1)}, bf16[1024,512]{0,1:T(8,128)(2,1)}, u32[]{:S(2)}) copy-start(bf16[1024,512]{0,1:T(8,128)(2,1)} %copy-done.3) | copy-start | bytes 3145732
  345.8 76.2 %copy-start.6 = (bf16[1024,512]{0,1:T(8,128)(2,1)S(1)}, bf16[1024,512]{0,1:T(8,128)(2,1)}, u32[]{:S(2)}) copy-start(bf16[1024,512]{0,1:T(8,128)(2,1)} %copy.21) | copy-start | bytes 3145732
  422.0 6.3 %copy-start.1 = (bf16[31,10000]{1,0:T(8,128)(2,1)S(1)}, bf16[31,10000]{1,0:T(8,128)(2,1)}, u32[]{:S(2)}) copy-start(bf16[31,10000]{1,0:T(8,128)(2,1)} %param.19) | copy-start | bytes 1860004
Sparse Core Ops, SparseCore 0:
  9.6 182.8 all-gather.2
  258.4 31.7 reduce-scatter.2
  293.5 51.0 reduce-scatter.4
where the time goes:
time: 438 us; the launch traced here: 437 us
  waiting for transfers between devices  237 us (54%)
  local copies, waits for them, and re-layouts  53.6 us (12%)
  blocking collectives  49 us (11%)
  matrix products  47.4 us (11%)
  other arithmetic  28.4 us (6%)
  between operations  18.5 us (4%)
    all_gather x1, waiting for transfers between devices, shards(): wind_piece = lax.all_gather(wind_dev, 'line', axis=1, tiled=True)  167 us
    reduce_scatter x1, waiting for transfers between devices, shards(): lax.psum_scatter(hessian_part, 'sample', scatter_dimension=1, tiled=True)  53.1 us
    psum x1, blocking collectives, shards(): lax.psum((jnp.sum(forward * forward), jnp.sum(gradient * gradient)), ('sa...  39.8 us
    gather x4, local copies, waits for them, and re-layouts, pick_buses(): jnp.take(wind_piece, jnp.clip(bus_ids, 0, piece_width - 1), axis=1)  20.7 us
    dot_general x1, matrix products, shards(): lax.dot_general(wind_piece, ptdf, (((1,), (1,)), ((), ())), preferred_ele...  17.1 us
    unnamed x28, local copies, waits for them, and re-layouts  15.8 us
    reduce_scatter x1, waiting for transfers between devices, shards(): lax.psum_scatter(gradient_part, 'sample', scatter_dimension=1, tiled=True)  15.7 us
    dot_general x1, matrix products, penalty_terms(): lax.dot_general(outer_prod, curve_term, (((0,), (0,)), ((), ())), precisi...  9.38 us
  transfers between devices with their start and end apart: 3, of which 3 were waited for; matrix products, arithmetic and copies ran while one was open for 8% of the time, Pallas kernels for 0%

commit v1 on v0

--- a/solution.py
+++ b/solution.py
@@ -110,7 +110,9 @@
         )
         return jnp.where(inside[None, :], picked, 0.0)
 
-    wind_piece = lax.all_gather(wind_dev, "line", axis=1, tiled=True)
+    wind_piece = jnp.concatenate(
+        lax.all_to_all(jnp.stack([wind_dev] * lax.axis_size("line")), "line", 0, 0), axis=1
+    )
     grid_flow = lax.dot_general(
         wind_piece, ptdf, (((1,), (1,)), ((), ())), preferred_element_type=jnp.float32
     )

time: 438 us -> 491 us (1.12)
  waiting for transfers between devices: 237 us -> 277 us
  starting transfers between devices: 0.12 us -> 6.52 us
  local copies, waits for them, and re-layouts: 53.6 us -> 59.9 us
    all_to_all x0 -> x1, waiting for transfers between devices: none -> 207 us  [shards(): lax.all_to_all(jnp.stack([wind_dev] * lax.axis_size('line')), 'line', 0, 0)]
    all_gather x1 -> x0, waiting for transfers between devices: 167 us -> none  [shards(): wind_piece = lax.all_gather(wind_dev, 'line', axis=1, tiled=True)]
    unnamed x28 -> x27, local copies, waits for them, and re-layouts: 15.8 us -> 4.33 us
    reshape x0 -> x1, local copies, waits for them, and re-layouts: none -> 11.5 us  [shards(): jnp.concatenate(lax.all_to_all(jnp.stack([wind_dev] * lax.axis_size('line...]
    all_to_all x0 -> x1, starting transfers between devices: none -> 6.48 us  [shards(): lax.all_to_all(jnp.stack([wind_dev] * lax.axis_size('line')), 'line', 0, 0)]
    another operation x0 -> x1, local copies, waits for them, and re-layouts: none -> 6.32 us  [shards(): jnp.stack([wind_dev] * lax.axis_size('line'))]
  transfers between devices with their start and end apart: 3 -> 3, of which waited for: 3 -> 3; matrix products, arithmetic and copies ran while one was open for 8% -> 7% of each run, Pallas kernels for 0% -> 0%
where the time goes in v1:
time: 491 us; the launch traced here: 490 us
  waiting for transfers between devices  277 us (56%)
  local copies, waits for them, and re-layouts  59.9 us (12%)
  blocking collectives  49 us (10%)
  matrix products  47.4 us (10%)
  other arithmetic  28.4 us (6%)
  between operations  18.8 us (4%)
  starting transfers between devices  6.52 us (1%)
    all_to_all x1, waiting for transfers between devices, shards(): lax.all_to_all(jnp.stack([wind_dev] * lax.axis_size('line')), 'line', 0, 0)  207 us
    reduce_scatter x1, waiting for transfers between devices, shards(): lax.psum_scatter(hessian_part, 'sample', scatter_dimension=1, tiled=True)  53.1 us
    psum x1, blocking collectives, shards(): lax.psum((jnp.sum(forward * forward), jnp.sum(gradient * gradient)), ('sa...  39.8 us
    gather x4, local copies, waits for them, and re-layouts, pick_buses(): jnp.take(wind_piece, jnp.clip(bus_ids, 0, piece_width - 1), axis=1)  20.7 us
    dot_general x1, matrix products, shards(): lax.dot_general(wind_piece, ptdf, (((1,), (1,)), ((), ())), preferred_ele...  17.1 us
    reduce_scatter x1, waiting for transfers between devices, shards(): lax.psum_scatter(gradient_part, 'sample', scatter_dimension=1, tiled=True)  16.6 us
    reshape x1, local copies, waits for them, and re-layouts, shards(): jnp.concatenate(lax.all_to_all(jnp.stack([wind_dev] * lax.axis_size('line...  11.5 us
  transfers between devices with their start and end apart: 3, of which 3 were waited for; matrix products, arithmetic and copies ran while one was open for 7% of the time, Pallas kernels for 0%

profile of v1, /device:TPU:0, one launch (start us, length us, event | category | flops | bytes accessed | tf_op | source)
XLA Modules:
  0.0 490.2 jit_solution(4977183389038718477)
XLA Ops:
  7.2 6.3 %stack.2 = bf16[4,512,2500]{1,2,0:T(8,128)(2,1)} broadcast(bf16[512,2500]{0,1:T(8,128)(2,1)} %param.17), dimensions={1,2} | broadcast | bytes 12800000 | tf_op jit(solution)/shard_map/stack | solution.py:114
  13.5 6.5 %all-to-all-start = ((bf16[4,512,2500]{1,2,0:T(8,128)(2,1)}), bf16[4,512,2500]{1,2,0:T(8,128)(2,1)}, u32[]{:S(2)}, u32[]{:S(2)}) async-start(bf16[4,512,2500]{1,2,0:T(8,128)(2,1)} %stack.2), calls=%async_computation | async-start | bytes 20512768 | tf_op jit(solution)/shard_map/all_to_all | solution.py:114
  20.0 4.3 copy.16
  24.3 5.7 %gather_fusion = s32[1024,2]{1,0:T(8,128)S(1)} fusion(s32[12706,2]{1,0:T(8,128)} %copy.16, s32[1024]{0:T(1024)S(1)} %fusion.32), kind=kCustom, calls=%fused_computation.2 | custom fusion | bytes 20480 | tf_op jit(solution)/shard_map/jit(_take)/gather | solution.py:98
  30.0 6.2 %gather_fusion.1 = f32[1024]{0:T(1024)S(1)} fusion(f32[12706]{0:T(1024)S(1)} %copy-done.2, s32[1024]{0:T(1024)S(1)} %fusion.32), kind=kCustom, calls=%fused_computation.3 | custom fusion | bytes 12288 | tf_op jit(solution)/shard_map/jit(_take)/gather | solution.py:101
  37.4 207.0 %all-to-all-done = bf16[4,512,2500]{1,2,0:T(8,128)(2,1)} async-done(((bf16[4,512,2500]{1,2,0:T(8,128)(2,1)}), bf16[4,512,2500]{1,2,0:T(8,128)(2,1)}, u32[]{:S(2)}, u32[]{:S(2)}) %all-to-all-start) | async-done | bytes 10240032 | tf_op jit(solution)/shard_map/all_to_all | solution.py:114
  244.5 11.5 %reshape.169 = bf16[512,10000]{0,1:T(8,128)(2,1)} reshape(bf16[512,4,2500]{0,2,1:T(8,128)(2,1)} %bitcast) | data formatting | bytes 20480000 | tf_op jit(solution)/shard_map/reshape | solution.py:113
  255.9 9.2 %gather_fusion.3 = bf16[1024,512]{1,0:T(8,128)(2,1)S(1)} fusion(bf16[512,10000]{0,1:T(8,128)(2,1)} %reshape.169, s32[1024]{0:T(1024)S(1)} %get-tuple-element.493), kind=kCustom, calls=%fused_computation.1.clone | custom fusion | bytes 2101248 | tf_op jit(solution)/shard_map/jit(_take)/gather | solution.py:108
  265.7 9.6 %gather_fusion.2 = bf16[1024,512]{1,0:T(8,128)(2,1)S(1)} fusion(bf16[512,10000]{0,1:T(8,128)(2,1)} %reshape.169, s32[1024]{0:T(1024)S(1)} %get-tuple-element.492), kind=kCustom, calls=%fused_computation.clone | custom fusion | bytes 2101248 | tf_op jit(solution)/shard_map/jit(_take)/gather | solution.py:108
  276.6 5.7 %fusion.37 = f32[512,31]{0,1:T(8,128)S(1)} fusion(bf16[512,10000]{0,1:T(8,128)(2,1)} %reshape.169, bf16[31,10000]{1,0:T(8,128)(2,1)S(1)} %copy-done), kind=kOutput, calls=%fused_computation.90 | convolution fusion | flops 317440000 | bytes 10923488 | tf_op jit(solution)/shard_map/dot_general | solution.py:121
  282.3 17.1 %fusion.38 = f32[512,1024]{1,0:T(8,128)S(1)} fusion(bf16[512,10000]{0,1:T(8,128)(2,1)} %reshape.169, bf16[1024,10000]{0,1:T(8,128)(2,1)} %param.18), kind=kOutput, calls=%fused_computation.91 | convolution fusion | flops 10485760000 | bytes 32817152 | tf_op jit(solution)/shard_map/dot_general | solution.py:116
  299.4 4.3 multiply_reduce_fusion.2
  303.8 2.2 fusion.27
  306.0 3.3 fusion.25
  313.6 9.4 %fusion.23 = f32[31,31,1024]{2,1,0:T(8,128)S(1)} fusion(f32[31,31,512]{2,1,0:T(8,128)S(1)} %dot_general.30, f32[512,1024]{1,0:T(8,128)} %copy-done.12, f32[1024]{0:T(1024)S(1)} %get-tuple-element.484), kind=kOutput, calls=%fused_computation.49 | convolution fusion | flops 6055002112 | bytes 8005632 | tf_op jit(solution)/shard_map/dot_general | solution.py:18
  323.9 2.4 bitcast_multiply_fusion.1
  326.4 16.6 %reduce-scatter.3.cloned.1.call-done = f32[32,128]{1,0:T(8,128)} async-done(((f32[32,1024]{1,0:T(8,128)}), f32[32,128]{1,0:T(8,128)}) %reduce-scatter.3.cloned.1.call-update) | async-done | bytes 16400 | tf_op jit(solution)/shard_map/reduce_scatter | solution.py:140
  344.3 53.1 %reduce-scatter.5.cloned.1.call-done = f32[1024,128]{1,0:T(8,128)} async-done(((f32[1024,1024]{1,0:T(8,128)}), f32[1024,128]{1,0:T(8,128)}) %reduce-scatter.5.cloned.1.call-update) | async-done | bytes 524304 | tf_op jit(solution)/shard_map/reduce_scatter | solution.py:139
  398.7 15.0 %while.51 = (s32[]{:T(128)}, f32[32,32,128]{2,1,0:T(8,128)S(1)}, f32[32,32,128]{2,1,0:T(8,128)S(1)}, s32[]{:T(128)}, s32[]{:T(128)}) while((s32[]{:T(128)}, f32[32,32,128]{2,1,0:T(8,128)S(1)}, f32[32,32,128]{2,1,0:T(8,128)S(1)}, s32[]{:T(128)}, s32[]{:T(128)}) %tuple.129), condition=%wide.region_4.6_spmd.clone.clone, body=%wide.region_2.5_spmd.clone.clone.sunk | while | flops 925923 | bytes 2787745 | solution.py:50
  413.7 4.2 while.49
  418.5 5.2 %while.50 = (s32[]{:T(128)}, f32[32,128]{1,0:T(8,128)S(1)}, f32[32,128]{1,0:T(8,128)S(1)}, f32[32,32,128]{2,1,0:T(8,128)S(1)}, s32[]{:T(128)}, /*index=5*/s32[]{:T(128)}, s32[]{:T(128)}, s32[]{:T(128)}) while((s32[]{:T(128)}, f32[32,128]{1,0:T(8,128)S(1)}, f32[32,128]{1,0:T(8,128)S(1)}, f32[32,32,128]{2,1,0:T(8,128)S(1)}, ...), condition=%wide.region_14.16_spmd.clone, body=%wide.region_12.15_spmd.clone.sunk | while | flops 24776 | bytes 101814 | solution.py:73
  423.7 9.2 %all_gather.3 = f32[32,1024]{1,0:T(8,128)S(1)} all-gather(f32[32,128]{1,0:T(8,128)S(1)} %neg.15), channel_id=1, replica_groups=mesh['sample'=8,'line'=4] {'sample'}, dimensions={1}, use_global_device_ids=true | all-gather | bytes 147456 | tf_op jit(solution)/shard_map/all_gather | solution.py:150
  433.0 39.8 %all-reduce = (f32[]{:T(128)}, f32[]{:T(128)}) all-reduce(f32[]{:T(128)} %multiply_reduce_fusion.5, f32[]{:T(128)} %get-tuple-element.482), channel_id=1, replica_groups=mesh['sample'=8,'line'=4] {'sample','line'}, use_global_device_ids=true, to_apply=%region_11.13 | all-reduce | flops 2 | bytes 16 | tf_op jit(solution)/shard_map/psum | solution.py:147
  474.9 5.5 %multiply_add_fusion.3 = f32[512,1024]{1,0:T(8,128)} fusion(f32[512,1024]{1,0:T(8,128)} %copy-done.12, f32[512,31]{0,1:T(8,128)S(1)} %fusion.37, f32[1024]{0:T(1024)S(1)} %bitcast.135, f32[]{:T(128)S(6)} %div.86, f32[32,1024]{1,0:T(8,128)S(1)} %all_gather.3, bf16[1024,512]{0,1:T(8,128)(2,1)S(1)} %copy-done.4, pred[1024]{0:T(1024)(128)(4,1)S(1)} %get-tuple-element.490, ...), kind=kOutput, calls=%fused_computation.51 | convolution fusion | flops 200802304 | bytes 6494212 | tf_op jit(solution)/shard_map/dot_general | solution.py:156
  (601 shorter events, 33.3 us)
Async XLA Ops:
  7.2 269.5 %copy-start = (bf16[31,10000]{1,0:T(8,128)(2,1)S(1)}, bf16[31,10000]{1,0:T(8,128)(2,1)}, u32[]{:S(2)}) copy-start(bf16[31,10000]{1,0:T(8,128)(2,1)} %param.19) | copy-start | bytes 1860004
  13.5 6.5 %copy-start.8 = (s32[12706,2]{0,1:T(2,128)S(1)}, s32[12706,2]{0,1:T(2,128)}, u32[]{:S(2)}) copy-start(s32[12706,2]{0,1:T(2,128)} %param.20) | copy-start | bytes 304948
  13.5 230.9 %all-to-all-start = ((bf16[4,512,2500]{1,2,0:T(8,128)(2,1)}), bf16[4,512,2500]{1,2,0:T(8,128)(2,1)}, u32[]{:S(2)}, u32[]{:S(2)}) async-start(bf16[4,512,2500]{1,2,0:T(8,128)(2,1)} %stack.2), calls=%async_computation | async-start | bytes 20512768 | tf_op jit(solution)/shard_map/all_to_all | solution.py:114
  20.0 4.3 copy-start.9
  20.0 323.0 %reduce-scatter.3.cloned.1.call-start = ((), (), s32[]{:S(2)}) async-start(), calls=%async_computation.3 | async-start | bytes 147456 | tf_op jit(solution)/shard_map/reduce_scatter | solution.py:140
  24.3 5.7 %copy-start.2 = (f32[12706]{0:T(1024)S(1)}, f32[12706]{0:T(1024)}, u32[]{:S(2)}) copy-start(f32[12706]{0:T(1024)} %param.22) | copy-start | bytes 152476
  29.9 6.2 %copy-start.7 = (f32[32,1024]{1,0:T(8,128)S(1)}, f32[32,1024]{1,0:T(8,128)}, u32[]{:S(2)}) copy-start(f32[32,1024]{1,0:T(8,128)} %param.25) | copy-start | bytes 393220
  36.1 1.3 copy-start.10
  265.7 40.3 %copy-start.3 = (bf16[1024,512]{0,1:T(8,128)(2,1)}, bf16[1024,512]{0,1:T(8,128)(2,1)S(1)}, u32[]{:S(2)}) copy-start(bf16[1024,512]{0,1:T(8,128)(2,1)S(1)} %copy.18) | copy-start | bytes 3145732
  282.3 17.1 %copy-start.5 = (bf16[1024,512]{0,1:T(8,128)(2,1)S(1)}, bf16[1024,512]{0,1:T(8,128)(2,1)}, u32[]{:S(2)}) copy-start(bf16[1024,512]{0,1:T(8,128)(2,1)} %copy.17) | copy-start | bytes 3145732
  282.3 17.1 %copy-start.11 = (f32[1024]{0:T(1024)S(1)}, f32[1024]{0:T(1024)}, u32[]{:S(2)}) copy-start(f32[1024]{0:T(1024)} %param.23) | copy-start | bytes 12292
  303.7 2.2 copy-start.12
  310.2 87.2 %reduce-scatter.5.cloned.1.call-start = ((), (), s32[]{:S(2)}) async-start(), calls=%async_computation.4 | async-start | bytes 4718592 | tf_op jit(solution)/shard_map/reduce_scatter | solution.py:139
  398.7 76.2 %copy-start.4 = (bf16[1024,512]{0,1:T(8,128)(2,1)S(1)}, bf16[1024,512]{0,1:T(8,128)(2,1)}, u32[]{:S(2)}) copy-start(bf16[1024,512]{0,1:T(8,128)(2,1)} %copy-done.3) | copy-start | bytes 3145732
  398.7 76.2 %copy-start.6 = (bf16[1024,512]{0,1:T(8,128)(2,1)S(1)}, bf16[1024,512]{0,1:T(8,128)(2,1)}, u32[]{:S(2)}) copy-start(bf16[1024,512]{0,1:T(8,128)(2,1)} %copy.17) | copy-start | bytes 3145732
  474.9 6.3 %copy-start.1 = (bf16[31,10000]{1,0:T(8,128)(2,1)S(1)}, bf16[31,10000]{1,0:T(8,128)(2,1)}, u32[]{:S(2)}) copy-start(bf16[31,10000]{1,0:T(8,128)(2,1)} %param.19) | copy-start | bytes 1860004
Sparse Core Ops, SparseCore 0:
  310.3 32.6 reduce-scatter.2
  346.3 51.0 reduce-scatter.4
